TPU v7x, 32 devices: a 4x4x1 block of a 4x4x8 slice. The times are simulated.
32 devices in a mesh: dp: 1 (over z), tp: 32 (over x, y, core).
Axes of the slice: x: 4, y: 4, z: 1, core: 2. Of those that a mesh axis runs over, the one named last changes fastest.
The devices are a block of a 4x4x8 slice.
Arguments:
- x: bfloat16 [2048, 5120], P('dp')
- w_gate: bfloat16 [5120, 16384], P(None, 'tp')
- w_up: bfloat16 [5120, 16384], P(None, 'tp')
- w_down: bfloat16 [16384, 5120], P('tp')
Outputs:
- output: bfloat16 [2048, 5120], P('dp')
All inputs are finite; a program needn't handle non-finite values.
Results may differ from a plain program's by a relative error of at most 0.016.
Values are sent between devices in bfloat16 or wider.
A program may use at most 768 MiB of HBM per device.

v0:
```python
import jax
import jax.numpy as jnp
from jax import lax
from jax.sharding import PartitionSpec as P


def solution(mesh):
    def step(x, w_gate, w_up, w_down):
        gate = jnp.dot(x, w_gate, preferred_element_type=jnp.float32)
        up = jnp.dot(x, w_up, preferred_element_type=jnp.float32)
        hidden = (jax.nn.silu(gate) * up).astype(jnp.bfloat16)
        term = jnp.dot(hidden, w_down, preferred_element_type=jnp.float32).astype(jnp.bfloat16)
        return lax.psum(term, "tp")

    return jax.shard_map(
        step,
        mesh=mesh,
        in_specs=(P("dp", None), P(None, "tp"), P(None, "tp"), P("tp", None)),
        out_specs=P("dp", None),
        check_vma=False,
    )
```

profile of v0, /device:TPU:97, one launch (start us, length us, event | category | flops | bytes accessed | tf_op | source)
XLA Modules:
  0.0 259.0 jit_solution(9610239468170194762)
XLA Ops:
  6.5 0.0 all-reduce.2.cloned.1.call-start
  6.6 0.0 copy-start
  6.6 15.7 %fusion = f32[2048,512]{1,0:T(8,128)S(1)} fusion(bf16[2048,5120]{1,0:T(8,128)(2,1)} %param.4, bf16[5120,512]{1,0:T(8,128)(2,1)} %param.5), kind=kOutput, calls=%fused_computation.2 | convolution fusion | flops 10737418240 | bytes 30408704 | tf_op jit(solution)/shard_map/dot_general | solution.py:9
  22.2 0.0 copy-done
  22.3 15.7 %multiply_convert_fusion = bf16[2048,512]{1,0:T(8,128)(2,1)S(1)} fusion(f32[2048,512]{1,0:T(8,128)S(1)} %fusion, bf16[2048,5120]{1,0:T(8,128)(2,1)} %param.4, bf16[5120,512]{1,0:T(8,128)(2,1)S(1)} %copy-done), kind=kOutput, calls=%fused_computation.1 | convolution fusion | flops 10743709696 | bytes 32505856 | tf_op jit(solution)/shard_map/dot_general | solution.py:10
  37.9 17.2 %convolution_convert_fusion = bf16[2048,5120]{1,0:T(8,128)(2,1)} fusion(bf16[2048,512]{1,0:T(8,128)(2,1)S(1)} %multiply_convert_fusion, bf16[512,5120]{1,0:T(8,128)(2,1)} %param.7), kind=kOutput, calls=%fused_computation | convolution fusion | flops 10747904000 | bytes 28311552 | tf_op jit(solution)/shard_map/dot_general | solution.py:12
  55.1 0.1 all-reduce.2.cloned.1.call-update
  55.2 179.7 %all-reduce.2.cloned.1.call-done = bf16[2048,5120]{1,0:T(8,128)(2,1)} async-done(((bf16[2048,5120]{1,0:T(8,128)(2,1)}), bf16[2048,5120]{1,0:T(8,128)(2,1)}) %all-reduce.2.cloned.1.call-update) | async-done | bytes 20971536 | tf_op jit(solution)/shard_map/psum | solution.py:13
  234.8 17.3 %copy.6 = bf16[2048,5120]{1,0:T(8,128)(2,1)} copy(bf16[2048,5120]{1,0:T(8,128)(2,1)} %all-reduce.2.cloned.1.call-done) | data formatting | bytes 41943040
Async XLA Ops:
  6.5 228.3 %all-reduce.2.cloned.1.call-start = ((), (), s32[]{:S(2)}) async-start(), calls=%async_computation | async-start | bytes 41943040 | tf_op jit(solution)/shard_map/psum | solution.py:13
  6.6 15.7 %copy-start = (bf16[5120,512]{1,0:T(8,128)(2,1)S(1)}, bf16[5120,512]{1,0:T(8,128)(2,1)}, u32[]{:S(2)}) copy-start(bf16[5120,512]{1,0:T(8,128)(2,1)} %param.6) | copy-start | bytes 15728644
Sparse Core Ops, SparseCore 0:
  55.3 179.5 all-reduce.1
where the time goes:
time: 259 us
  waiting for transfers between devices  180 us (69%)
  matrix products  48.5 us (19%)
  local copies, waits for them, and re-layouts  17.3 us (7%)
  between operations  13.4 us (5%)
    psum x1, waiting for transfers between devices, step(): return lax.psum(term, 'tp')  180 us
    unnamed x3, local copies, waits for them, and re-layouts  17.3 us
    dot_general x1, matrix products, step(): jnp.dot(hidden, w_down, preferred_element_type=jnp.float32)  17.2 us
    dot_general x1, matrix products, step(): gate = jnp.dot(x, w_gate, preferred_element_type=jnp.float32)  15.7 us
    dot_general x1, matrix products, step(): up = jnp.dot(x, w_up, preferred_element_type=jnp.float32)  15.7 us
  transfers between devices with their start and end apart: 1, of which 1 were waited for; matrix products, arithmetic and copies ran while one was open for 0% of the time, Pallas kernels for 0%

commit v1 on v0

v1 whole, which is shorter than its diff:
```python
import functools
import math

import jax
import jax.numpy as jnp
from jax import lax
from jax.experimental import pallas as pl
from jax.experimental.pallas import tpu as pltpu
from jax.sharding import PartitionSpec as P

MESH = pl.DeviceIdType.MESH
ROWS = 128
KSLICES = 5
F32, BF16 = jnp.float32, jnp.bfloat16


def _kernel(
    side, nc, x_hbm, wg_hbm, wu_hbm, wd_hbm, y,
    wg, wu, wd, xb, h, p32, p16, got1, got2, fw1, fw2, t32, t16,
    s1, r1, s2, r2, sg2, rg2, sg1, rg1, sd, rd, sh, rh, swd, rwd, lx, lw, lwd,
):
    R = xb.shape[1]
    K = xb.shape[2]
    FF = wg.shape[1]
    C = p32.shape[2]
    CB, CH = C // 2, C // 4
    R1, R2 = R // side, R // side // side

    me = lax.axis_index("tp")
    core = lax.rem(me, 2)
    chip = lax.div(me, 2)
    cx, cy = lax.div(chip, side), lax.rem(chip, side)
    mate = me + 1 - 2 * core

    def dev(a, b):
        return (lax.rem(a + side, side) * side + lax.rem(b + side, side)) * 2 + core

    xp, xm, yp, ym = dev(cx + 1, cy), dev(cx - 1, cy), dev(cx, cy + 1), dev(cx, cy - 1)
    ring = {
        1: ((cx, xp, xm), (cy, yp, ym)),
        2: ((cy, yp, ym), (cx, xp, xm)),
    }

    def remote(src, dst, ssem, rsem, to):
        return pltpu.make_async_remote_copy(
            src_ref=src, dst_ref=dst, send_sem=ssem, recv_sem=rsem,
            device_id={"tp": to}, device_id_type=MESH,
        )

    def load_x(j):
        rows = pl.ds(pl.multiple_of(j * R, R), R)
        slot = lax.rem(j, 2)
        return pltpu.make_async_copy(x_hbm.at[rows, :], xb.at[slot], lx.at[slot])

    KS = K // KSLICES

    def load_w(i):
        rows = pl.ds(i * KS, KS)
        return (
            pltpu.make_async_copy(wg_hbm.at[rows, :], wg.at[rows, :], lw.at[0, i]),
            pltpu.make_async_copy(wu_hbm.at[rows, :], wu.at[rows, :], lw.at[1, i]),
        )

    my_cols = pl.ds(pl.multiple_of(core * C, C), C)
    mate_cols = pl.ds(pl.multiple_of((1 - core) * C, C), C)

    load_x(0).start()
    for i in range(KSLICES):
        for copy in load_w(i):
            copy.start()
    wd_own = pltpu.make_async_copy(wd_hbm.at[:, my_cols], wd.at[pl.ds(0, FF), :], lwd)
    wd_own.start()
    load_x(1).start()

    barrier = pltpu.get_barrier_semaphore()
    for d in (mate, xp, xm, yp, ym):
        pl.semaphore_signal(barrier, inc=1, device_id={"tp": d}, device_id_type=MESH)
    pl.semaphore_wait(barrier, 5)

    wd_mate = remote(wd_hbm.at[:, mate_cols], wd.at[pl.ds(FF, FF), :], swd, rwd, mate)
    wd_mate.start()

    def send_h(j):
        return remote(
            h.at[j, :, pl.ds(0, FF)], h.at[j, :, pl.ds(FF, FF)], sh.at[j], rh.at[j], mate
        )

    TN = min(256, FF)

    def gate_up(j):
        slot = lax.rem(j, 2)
        load_x(j).wait()
        for t in range(FF // TN):
            cols = pl.ds(t * TN, TN)
            g = jnp.dot(xb[slot], wg[:, cols], preferred_element_type=F32)
            u = jnp.dot(xb[slot], wu[:, cols], preferred_element_type=F32)
            h[j, :, cols] = (jax.nn.silu(g) * u).astype(BF16)
        send_h(j).start()

        @pl.when(j + 2 < nc)
        def _():
            load_x(j + 2).start()

    def gate_up_first():
        load_x(0).wait()
        for i in range(KSLICES):
            for copy in load_w(i):
                copy.wait()
            part = pl.ds(i * KS, KS)
            g = jnp.dot(xb[0, :, part], wg[part, :], preferred_element_type=F32)
            u = jnp.dot(xb[0, :, part], wu[part, :], preferred_element_type=F32)
            if i > 0:
                g, u = p32[0, :, pl.ds(0, FF)] + g, p32[1, :, pl.ds(0, FF)] + u
            if i < KSLICES - 1:
                p32[0, :, pl.ds(0, FF)] = g
                p32[1, :, pl.ds(0, FF)] = u
            else:
                h[0, :, pl.ds(0, FF)] = (jax.nn.silu(g) * u).astype(BF16)
        send_h(0).start()
        load_x(2).start()

    TD = 512 if C % 512 == 0 else CH

    def down(j):
        slot = lax.rem(j, 2)
        send_h(j).wait()
        for t in range(C // TD):
            cols = pl.ds(t * TD, TD)
            p = jnp.dot(h[j], wd[:, cols], preferred_element_type=F32)
            p32[slot, :, cols] = p
            p16[slot, :, cols] = p.astype(BF16)

    def piece(phase, q):
        size = R1 if phase == 1 else R2
        return pl.ds(pl.multiple_of(lax.rem(q + side, side) * size, size), size)

    def half(phase, k, hf):
        return pl.ds((k * CB if phase == 1 else 0) + hf * CH, CH)

    def term(phase, j, k, q, hf, wide):
        slot = lax.rem(j, 2)
        where = (piece(phase, q), half(phase, k, hf))
        if phase == 1:
            return (p32 if wide else p16).at[slot, *where]
        return (t32 if wide else t16).at[slot, k, *where]

    bufs = {1: (got1, fw1, s1, r1), 2: (got2, fw2, s2, r2)}

    def message(phase, j, k, m):
        got, fw, ss, rs = bufs[phase]
        q, np_, nm = ring[phase][k]
        slot = lax.rem(j, 2)
        if m < 4:
            dq, hf, to = ((2, 0, np_), (2, 1, nm), (1, 1, np_), (-1, 0, nm))[m]
            src = term(phase, j, k, q + dq, hf, False)
        else:
            src, to = fw.at[slot, k, m - 4], (np_, nm)[m - 4]
        return remote(src, got.at[j, k, m], ss.at[slot, k, m], rs.at[j, k, m], to)

    def rs_raw(phase, j):
        for m in range(4):
            for k in range(2):
                message(phase, j, k, m).start()

    def rs_forward(phase, j):
        got, fw, _, _ = bufs[phase]
        slot = lax.rem(j, 2)
        for hf in range(2):
            for k in range(2):
                q, _, _ = ring[phase][k]
                message(phase, j, k, hf).wait_recv()
                qq = q + 1 if hf == 0 else q - 1
                total = term(phase, j, k, qq, hf, True)[...] + got[j, k, hf].astype(F32)
                fw[slot, k, hf] = total.astype(BF16)
                message(phase, j, k, 4 + hf).start()

    def rs_finish(phase, j, store):
        got, _, _, _ = bufs[phase]
        for k in range(2):
            q, _, _ = ring[phase][k]
            for hf in range(2):
                message(phase, j, k, 4 + hf).wait_recv()
                message(phase, j, k, 3 - hf).wait_recv()
                total = (
                    term(phase, j, k, q, hf, True)[...]
                    + got[j, k, 4 + hf].astype(F32)
                    + got[j, k, 3 - hf].astype(F32)
                )
                store(k, hf, total)
        for k in range(2):
            for m in range(6):
                message(phase, j, k, m).wait_send()

    def store_t(j):
        slot = lax.rem(j, 2)

        def store(k, hf, total):
            t32[slot, k, :, pl.ds(hf * CH, CH)] = total
            t16[slot, k, :, pl.ds(hf * CH, CH)] = total.astype(BF16)

        return store

    def y_block(phase, j, k, q, hf=None):
        q1 = ring[1][k][0]
        col = core * C + k * CB + (0 if hf is None else hf * CH)
        cols = pl.ds(pl.multiple_of(col, CH), CB if hf is None else CH)
        if phase == 2:
            row = j * R + q1 * R1 + lax.rem(q + side, side) * R2
            return y.at[pl.ds(pl.multiple_of(row, R2), R2), cols]
        row = j * R + lax.rem(q + side, side) * R1
        return y.at[pl.ds(pl.multiple_of(row, R1), R1), cols]

    gsem = {1: (sg1, rg1), 2: (sg2, rg2)}

    def gather(phase, j, k, m, got):
        ss, rs = gsem[phase]
        q, np_, nm = ring[phase][k]
        dq, hf = (((-1, None), (1, None), (-2, 0), (2, 1)) if got else ((0, None), (0, None), (-1, 0), (1, 1)))[m]
        block = y_block(phase, j, k, q + dq, hf)
        return remote(block, block, ss.at[lax.rem(j, 2), k, m], rs.at[j, k, m], (np_, nm)[m % 2])

    def ag_start(phase, j):
        for m in range(2):
            for k in range(2):
                gather(phase, j, k, m, False).start()

    def ag_pass(phase, j):
        for m in range(2):
            for k in range(2):
                gather(phase, j, k, m, True).wait_recv()
                gather(phase, j, k, 2 + m, False).start()

    def ag_end(phase, j):
        for m in range(2, 4):
            for k in range(2):
                gather(phase, j, k, m, True).wait_recv()
        for k in range(2):
            for m in range(4):
                gather(phase, j, k, m, False).wait_send()

    def swap(j, mine):
        rows = pl.ds(pl.multiple_of(j * R, R), R)
        block = y.at[rows, my_cols if mine else mate_cols]
        return remote(block, block, sd.at[lax.rem(j, 2)], rd.at[j], mate)

    def stage2(j):
        rs_finish(1, j, store_t(j))
        rs_raw(2, j)

    def stage4(j):
        def store(k, hf, total):
            q2 = ring[2][k][0]
            y_block(2, j, k, q2, hf)[...] = total.astype(BF16)

        rs_finish(2, j, store)
        ag_start(2, j)

    def stage6(j):
        ag_end(2, j)
        ag_start(1, j)

    def stage8(j):
        ag_end(1, j)
        swap(j, True).start()

    def stage9(j):
        swap(j, True).wait_send()
        swap(j, False).wait_recv()

    stages = (
        None,
        functools.partial(rs_forward, 1),
        stage2,
        functools.partial(rs_forward, 2),
        stage4,
        functools.partial(ag_pass, 2),
        stage6,
        functools.partial(ag_pass, 1),
        stage8,
        stage9,
    )

    gate_up_first()
    wd_own.wait()
    wd_mate.wait()

    def step(s, carry):
        for lag in range(len(stages) - 1, 0, -1):
            j = s - lag

            @pl.when(jnp.logical_and(j >= 0, j < nc))
            def _():
                stages[lag](j)

        @pl.when(s < nc)
        def _():
            down(s)
            rs_raw(1, s)

        @pl.when(s + 1 < nc)
        def _():
            gate_up(s + 1)

        return carry

    lax.fori_loop(0, nc + len(stages) - 1, step, 0)


def _mlp(side, x, w_gate, w_up, w_down):
    rows, depth = x.shape
    ff = w_gate.shape[1]
    width = w_down.shape[1]
    C = width // 2
    R = ROWS
    nc = rows // R
    CB, CH = C // 2, C // 4
    R1, R2 = R // side, R // side // side
    dma = pltpu.SemaphoreType.DMA
    y = pl.pallas_call(
        functools.partial(_kernel, side, nc),
        out_shape=pltpu.VMEM((rows, width), BF16),
        in_specs=[pl.BlockSpec(memory_space=pl.ANY)] * 4,
        out_specs=pl.BlockSpec(memory_space=pltpu.VMEM),
        scratch_shapes=[
            pltpu.VMEM((depth, ff), BF16),
            pltpu.VMEM((depth, ff), BF16),
            pltpu.VMEM((2 * ff, C), BF16),
            pltpu.VMEM((2, R, depth), BF16),
            pltpu.VMEM((nc, R, 2 * ff), BF16),
            pltpu.VMEM((2, R, C), F32),
            pltpu.VMEM((2, R, C), BF16),
            pltpu.VMEM((nc, 2, 6, R1, CH), BF16),
            pltpu.VMEM((nc, 2, 6, R2, CH), BF16),
            pltpu.VMEM((2, 2, 2, R1, CH), BF16),
            pltpu.VMEM((2, 2, 2, R2, CH), BF16),
            pltpu.VMEM((2, 2, R1, CB), F32),
            pltpu.VMEM((2, 2, R1, CB), BF16),
            dma((2, 2, 6)), dma((nc, 2, 6)),
            dma((2, 2, 6)), dma((nc, 2, 6)),
            dma((2, 2, 4)), dma((nc, 2, 4)),
            dma((2, 2, 4)), dma((nc, 2, 4)),
            dma((2,)), dma((nc,)),
            dma((nc,)), dma((nc,)),
            dma, dma,
            dma((2,)), dma((2, KSLICES)), dma,
        ],
        compiler_params=pltpu.CompilerParams(
            collective_id=0, has_side_effects=True, vmem_limit_bytes=43 * 1024 * 1024,
        ),
        cost_estimate=pl.CostEstimate(
            flops=6 * rows * depth * ff, bytes_accessed=4 * rows * depth, transcendentals=rows * ff,
        ),
    )(x, w_gate, w_up, w_down)
    return y


def solution(mesh):
    side = math.isqrt(mesh.shape["tp"] // 2)

    return jax.shard_map(
        functools.partial(_mlp, side),
        mesh=mesh,
        in_specs=(P("dp", None), P(None, "tp"), P(None, "tp"), P("tp", None)),
        out_specs=P("dp", None),
        check_vma=False,
    )
```

time: 259 us -> 154 us (0.59)
  waiting for transfers between devices: 180 us -> 0 us
  Pallas kernels: 0 us -> 147 us
  matrix products: 48.5 us -> 0 us
  between operations: 13.4 us -> 0.01 us
  local copies, waits for them, and re-layouts: 17.3 us -> 7.54 us
    psum x1 -> x0, waiting for transfers between devices: 180 us -> none  [step(): return lax.psum(term, 'tp')]
    pallas_call x0 -> x1, Pallas kernels: none -> 147 us  [_mlp(): pl.pallas_call(functools.partial(_kernel, side, nc), out_shape=pltpu.VMEM...]
    dot_general x3 -> x0, matrix products: 48.5 us -> none  [the longest x1 17.2 us: step(): jnp.dot(hidden, w_down, preferred_element_type=jnp.float32)]
    unnamed x3 -> x1, local copies, waits for them, and re-layouts: 17.3 us -> 7.54 us
  transfers between devices with their start and end apart: 1 -> 0, of which waited for: 1 -> 0; matrix products, arithmetic and copies ran while one was open for 0% -> 0% of each run, Pallas kernels for 0% -> 0%
where the time goes in v1:
time: 154 us
  Pallas kernels  147 us (95%)
  local copies, waits for them, and re-layouts  7.54 us (5%)
    pallas_call x1, Pallas kernels, _mlp(): pl.pallas_call(functools.partial(_kernel, side, nc), out_shape=pltpu.VMEM...  147 us
    unnamed x1, local copies, waits for them, and re-layouts  7.54 us

profile of v1, /device:TPU:97, one launch (start us, length us, event | category | flops | bytes accessed | tf_op | source)
XLA Modules:
  0.0 154.2 jit_solution(8752257543841984408)
XLA Ops:
  0.0 146.6 %shard_map.46 = bf16[2048,5120]{1,0:T(8,128)(2,1)S(1)} custom-call(bf16[2048,5120]{1,0:T(8,128)(2,1)} %x_hbm.1, bf16[5120,512]{1,0:T(8,128)(2,1)} %wg_hbm.1, bf16[5120,512]{1,0:T(8,128)(2,1)} %wu_hbm.1, bf16[512,5120]{1,0:T(8,128)(2,1)} %wd_hbm.1), custom_call_target="tpu_custom_call" | custom-call | flops 32212254720 | bytes 41943040 | tf_op jit(solution)/shard_map/pallas_call | solution.py:319
  146.6 7.5 %copy.6 = bf16[2048,5120]{1,0:T(8,128)(2,1)} copy(bf16[2048,5120]{1,0:T(8,128)(2,1)S(1)} %shard_map.46) | data formatting | bytes 41943040

commit v2 on v1

--- a/solution.py
+++ b/solution.py
@@ -11,13 +11,15 @@
 MESH = pl.DeviceIdType.MESH
 ROWS = 128
 KSLICES = 5
+LAGS = (0, 2, 4, 6, 8, 10, 14, 16, 18, 20)
+SLOTS = 8
 F32, BF16 = jnp.float32, jnp.bfloat16
 
 
 def _kernel(
     side, nc, x_hbm, wg_hbm, wu_hbm, wd_hbm, y,
     wg, wu, wd, xb, h, p32, p16, got1, got2, fw1, fw2, t32, t16,
-    s1, r1, s2, r2, sg2, rg2, sg1, rg1, sd, rd, sh, rh, swd, rwd, lx, lw, lwd,
+    s1a, s1b, r1a, r1b, s2a, s2b, r2a, r2b, sg2a, sg2b, rg2a, rg2b, sg1a, sg1b, rg1a, rg1b, sd, rd, sh, rh, swd, rwd, lx, lw, lwd,
 ):
     R = xb.shape[1]
     K = xb.shape[2]
@@ -47,6 +49,9 @@
             device_id={"tp": to}, device_id_type=MESH,
         )
 
+    def turn(ref, j):
+        return lax.rem(j, ref.shape[0])
+
     def load_x(j):
         rows = pl.ds(pl.multiple_of(j * R, R), R)
         slot = lax.rem(j, 2)
@@ -82,7 +87,8 @@
 
     def send_h(j):
         return remote(
-            h.at[j, :, pl.ds(0, FF)], h.at[j, :, pl.ds(FF, FF)], sh.at[j], rh.at[j], mate
+            h.at[turn(h, j), :, pl.ds(0, FF)], h.at[turn(h, j), :, pl.ds(FF, FF)],
+            sh.at[turn(sh, j)], rh.at[turn(rh, j)], mate,
         )
 
     TN = min(256, FF)
@@ -94,7 +100,7 @@
             cols = pl.ds(t * TN, TN)
             g = jnp.dot(xb[slot], wg[:, cols], preferred_element_type=F32)
             u = jnp.dot(xb[slot], wu[:, cols], preferred_element_type=F32)
-            h[j, :, cols] = (jax.nn.silu(g) * u).astype(BF16)
+            h[turn(h, j), :, cols] = (jax.nn.silu(g) * u).astype(BF16)
         send_h(j).start()
 
         @pl.when(j + 2 < nc)
@@ -122,13 +128,12 @@
     TD = 512 if C % 512 == 0 else CH
 
     def down(j):
-        slot = lax.rem(j, 2)
         send_h(j).wait()
         for t in range(C // TD):
             cols = pl.ds(t * TD, TD)
-            p = jnp.dot(h[j], wd[:, cols], preferred_element_type=F32)
-            p32[slot, :, cols] = p
-            p16[slot, :, cols] = p.astype(BF16)
+            p = jnp.dot(h[turn(h, j)], wd[:, cols], preferred_element_type=F32)
+            p32[turn(p32, j), :, cols] = p
+            p16[turn(p16, j), :, cols] = p.astype(BF16)
 
     def piece(phase, q):
         size = R1 if phase == 1 else R2
@@ -138,24 +143,32 @@
         return pl.ds((k * CB if phase == 1 else 0) + hf * CH, CH)
 
     def term(phase, j, k, q, hf, wide):
-        slot = lax.rem(j, 2)
         where = (piece(phase, q), half(phase, k, hf))
         if phase == 1:
-            return (p32 if wide else p16).at[slot, *where]
-        return (t32 if wide else t16).at[slot, k, *where]
-
-    bufs = {1: (got1, fw1, s1, r1), 2: (got2, fw2, s2, r2)}
+            ref = p32 if wide else p16
+            return ref.at[turn(ref, j), *where]
+        ref = t32 if wide else t16
+        return ref.at[turn(ref, j), k, *where]
+
+    bufs = {1: (got1, fw1, (s1a, s1b), (r1a, r1b)), 2: (got2, fw2, (s2a, s2b), (r2a, r2b))}
 
     def message(phase, j, k, m):
         got, fw, ss, rs = bufs[phase]
         q, np_, nm = ring[phase][k]
-        slot = lax.rem(j, 2)
         if m < 4:
             dq, hf, to = ((2, 0, np_), (2, 1, nm), (1, 1, np_), (-1, 0, nm))[m]
             src = term(phase, j, k, q + dq, hf, False)
         else:
-            src, to = fw.at[slot, k, m - 4], (np_, nm)[m - 4]
-        return remote(src, got.at[j, k, m], ss.at[slot, k, m], rs.at[j, k, m], to)
+            src, to = fw.at[turn(fw, j), k, m - 4], (np_, nm)[m - 4]
+        return remote(
+            src, got.at[turn(got, j), m, k],
+            ss[m // 4].at[turn(ss[m // 4], j)], rs[m // 2 > 0].at[turn(rs[m // 2 > 0], j)], to,
+        )
+
+    def messages(phase, j, lo, hi):
+        got, _, ss, rs = bufs[phase]
+        block = got.at[turn(got, j), pl.ds(lo, hi - lo)]
+        return remote(block, block, ss[lo // 4].at[turn(ss[lo // 4], j)], rs[lo // 2 > 0].at[turn(rs[lo // 2 > 0], j)], mate)
 
     def rs_raw(phase, j):
         for m in range(4):
@@ -164,39 +177,34 @@
 
     def rs_forward(phase, j):
         got, fw, _, _ = bufs[phase]
-        slot = lax.rem(j, 2)
+        messages(phase, j, 0, 2).wait_recv()
         for hf in range(2):
             for k in range(2):
                 q, _, _ = ring[phase][k]
-                message(phase, j, k, hf).wait_recv()
                 qq = q + 1 if hf == 0 else q - 1
-                total = term(phase, j, k, qq, hf, True)[...] + got[j, k, hf].astype(F32)
-                fw[slot, k, hf] = total.astype(BF16)
+                total = term(phase, j, k, qq, hf, True)[...] + got[turn(got, j), hf, k].astype(F32)
+                fw[turn(fw, j), k, hf] = total.astype(BF16)
                 message(phase, j, k, 4 + hf).start()
+        messages(phase, j, 0, 4).wait_send()
 
     def rs_finish(phase, j, store):
         got, _, _, _ = bufs[phase]
+        messages(phase, j, 2, 6).wait_recv()
         for k in range(2):
             q, _, _ = ring[phase][k]
             for hf in range(2):
-                message(phase, j, k, 4 + hf).wait_recv()
-                message(phase, j, k, 3 - hf).wait_recv()
                 total = (
                     term(phase, j, k, q, hf, True)[...]
-                    + got[j, k, 4 + hf].astype(F32)
-                    + got[j, k, 3 - hf].astype(F32)
+                    + got[turn(got, j), 4 + hf, k].astype(F32)
+                    + got[turn(got, j), 3 - hf, k].astype(F32)
                 )
                 store(k, hf, total)
-        for k in range(2):
-            for m in range(6):
-                message(phase, j, k, m).wait_send()
+        messages(phase, j, 4, 6).wait_send()
 
     def store_t(j):
-        slot = lax.rem(j, 2)
-
         def store(k, hf, total):
-            t32[slot, k, :, pl.ds(hf * CH, CH)] = total
-            t16[slot, k, :, pl.ds(hf * CH, CH)] = total.astype(BF16)
+            t32[turn(t32, j), k, :, pl.ds(hf * CH, CH)] = total
+            t16[turn(t16, j), k, :, pl.ds(hf * CH, CH)] = total.astype(BF16)
 
         return store
 
@@ -210,38 +218,41 @@
         row = j * R + lax.rem(q + side, side) * R1
         return y.at[pl.ds(pl.multiple_of(row, R1), R1), cols]
 
-    gsem = {1: (sg1, rg1), 2: (sg2, rg2)}
-
-    def gather(phase, j, k, m, got):
-        ss, rs = gsem[phase]
+    gsem = {1: ((sg1a, sg1b), (rg1a, rg1b)), 2: ((sg2a, sg2b), (rg2a, rg2b))}
+
+    def gather(phase, j, k, m):
+        ss, rs = (sems[m // 2] for sems in gsem[phase])
         q, np_, nm = ring[phase][k]
-        dq, hf = (((-1, None), (1, None), (-2, 0), (2, 1)) if got else ((0, None), (0, None), (-1, 0), (1, 1)))[m]
+        dq, hf = ((0, None), (0, None), (-1, 0), (1, 1))[m]
         block = y_block(phase, j, k, q + dq, hf)
-        return remote(block, block, ss.at[lax.rem(j, 2), k, m], rs.at[j, k, m], (np_, nm)[m % 2])
+        return remote(block, block, ss.at[turn(ss, j)], rs.at[turn(rs, j)], (np_, nm)[m % 2])
+
+    def gathers(phase, j, late):
+        ss, rs = (sems[late] for sems in gsem[phase])
+        size = (R1, R)[phase == 1] // (1 + late)
+        block = y.at[pl.ds(pl.multiple_of(j * R, R), size), pl.ds(0, CB)]
+        return remote(block, block, ss.at[turn(ss, j)], rs.at[turn(rs, j)], mate)
 
     def ag_start(phase, j):
         for m in range(2):
             for k in range(2):
-                gather(phase, j, k, m, False).start()
+                gather(phase, j, k, m).start()
 
     def ag_pass(phase, j):
+        gathers(phase, j, 0).wait_recv()
         for m in range(2):
             for k in range(2):
-                gather(phase, j, k, m, True).wait_recv()
-                gather(phase, j, k, 2 + m, False).start()
+                gather(phase, j, k, 2 + m).start()
+        gathers(phase, j, 0).wait_send()
 
     def ag_end(phase, j):
-        for m in range(2, 4):
-            for k in range(2):
-                gather(phase, j, k, m, True).wait_recv()
-        for k in range(2):
-            for m in range(4):
-                gather(phase, j, k, m, False).wait_send()
+        gathers(phase, j, 1).wait_recv()
+        gathers(phase, j, 1).wait_send()
 
     def swap(j, mine):
         rows = pl.ds(pl.multiple_of(j * R, R), R)
         block = y.at[rows, my_cols if mine else mate_cols]
-        return remote(block, block, sd.at[lax.rem(j, 2)], rd.at[j], mate)
+        return remote(block, block, sd.at[turn(sd, j)], rd.at[turn(rd, j)], mate)
 
     def stage2(j):
         rs_finish(1, j, store_t(j))
@@ -285,25 +296,25 @@
     wd_mate.wait()
 
     def step(s, carry):
-        for lag in range(len(stages) - 1, 0, -1):
-            j = s - lag
+        for i in range(len(stages) - 1, 0, -1):
+            j = s - LAGS[i]
 
             @pl.when(jnp.logical_and(j >= 0, j < nc))
             def _():
-                stages[lag](j)
+                stages[i](j)
+
+        @pl.when(s + 1 < nc)
+        def _():
+            gate_up(s + 1)
 
         @pl.when(s < nc)
         def _():
             down(s)
             rs_raw(1, s)
 
-        @pl.when(s + 1 < nc)
-        def _():
-            gate_up(s + 1)
-
         return carry
 
-    lax.fori_loop(0, nc + len(stages) - 1, step, 0)
+    lax.fori_loop(0, nc + LAGS[-1], step, 0)
 
 
 def _mlp(side, x, w_gate, w_up, w_down):
@@ -315,6 +326,7 @@
     nc = rows // R
     CB, CH = C // 2, C // 4
     R1, R2 = R // side, R // side // side
+    L = LAGS
     dma = pltpu.SemaphoreType.DMA
     y = pl.pallas_call(
         functools.partial(_kernel, side, nc),
@@ -326,21 +338,21 @@
             pltpu.VMEM((depth, ff), BF16),
             pltpu.VMEM((2 * ff, C), BF16),
             pltpu.VMEM((2, R, depth), BF16),
-            pltpu.VMEM((nc, R, 2 * ff), BF16),
-            pltpu.VMEM((2, R, C), F32),
-            pltpu.VMEM((2, R, C), BF16),
-            pltpu.VMEM((nc, 2, 6, R1, CH), BF16),
-            pltpu.VMEM((nc, 2, 6, R2, CH), BF16),
-            pltpu.VMEM((2, 2, 2, R1, CH), BF16),
-            pltpu.VMEM((2, 2, 2, R2, CH), BF16),
-            pltpu.VMEM((2, 2, R1, CB), F32),
-            pltpu.VMEM((2, 2, R1, CB), BF16),
-            dma((2, 2, 6)), dma((nc, 2, 6)),
-            dma((2, 2, 6)), dma((nc, 2, 6)),
-            dma((2, 2, 4)), dma((nc, 2, 4)),
-            dma((2, 2, 4)), dma((nc, 2, 4)),
-            dma((2,)), dma((nc,)),
-            dma((nc,)), dma((nc,)),
+            pltpu.VMEM((4, R, 2 * ff), BF16),
+            pltpu.VMEM((L[2], R, C), F32),
+            pltpu.VMEM((L[1], R, C), BF16),
+            pltpu.VMEM((SLOTS, 6, 2, R1, CH), BF16),
+            pltpu.VMEM((SLOTS, 6, 2, R2, CH), BF16),
+            pltpu.VMEM((L[2] - L[1], 2, 2, R1, CH), BF16),
+            pltpu.VMEM((L[4] - L[3], 2, 2, R2, CH), BF16),
+            pltpu.VMEM((L[4] - L[2], 2, R1, CB), F32),
+            pltpu.VMEM((L[3] - L[2], 2, R1, CB), BF16),
+            dma((L[1],)), dma((L[2] - L[1],)), dma((SLOTS,)), dma((SLOTS,)),
+            dma((L[3] - L[2],)), dma((L[4] - L[3],)), dma((SLOTS,)), dma((SLOTS,)),
+            dma((L[5] - L[4],)), dma((L[6] - L[5],)), dma((SLOTS,)), dma((SLOTS,)),
+            dma((L[7] - L[6],)), dma((L[8] - L[7],)), dma((SLOTS,)), dma((SLOTS,)),
+            dma((L[9] - L[8],)), dma((SLOTS,)),
+            dma((2,)), dma((4,)),
             dma, dma,
             dma((2,)), dma((2, KSLICES)), dma,
         ],

time: 154 us -> 137 us (0.89)
  Pallas kernels: 147 us -> 130 us
    pallas_call x1, Pallas kernels: 147 us -> 130 us  [_mlp(): pl.pallas_call(functools.partial(_kernel, side, nc), out_shape=pltpu.VMEM...]
where the time goes in v2:
time: 137 us
  Pallas kernels  130 us (95%)
  local copies, waits for them, and re-layouts  7.54 us (6%)
    pallas_call x1, Pallas kernels, _mlp(): pl.pallas_call(functools.partial(_kernel, side, nc), out_shape=pltpu.VMEM...  130 us
    unnamed x1, local copies, waits for them, and re-layouts  7.54 us

profile of v2, /device:TPU:97, one launch (start us, length us, event | category | flops | bytes accessed | tf_op | source)
XLA Modules:
  0.0 137.1 jit_solution(12055099869128884284)
XLA Ops:
  0.0 129.5 %shard_map.46 = bf16[2048,5120]{1,0:T(8,128)(2,1)S(1)} custom-call(bf16[2048,5120]{1,0:T(8,128)(2,1)} %x_hbm.1, bf16[5120,512]{1,0:T(8,128)(2,1)} %wg_hbm.1, bf16[5120,512]{1,0:T(8,128)(2,1)} %wu_hbm.1, bf16[512,5120]{1,0:T(8,128)(2,1)} %wd_hbm.1), custom_call_target="tpu_custom_call" | custom-call | flops 32212254720 | bytes 41943040 | tf_op jit(solution)/shard_map/pallas_call | solution.py:331
  129.5 7.5 %copy.6 = bf16[2048,5120]{1,0:T(8,128)(2,1)} copy(bf16[2048,5120]{1,0:T(8,128)(2,1)S(1)} %shard_map.46) | data formatting | bytes 41943040

commit v3 on v2

--- a/solution.py
+++ b/solution.py
@@ -10,20 +10,22 @@
 
 MESH = pl.DeviceIdType.MESH
 ROWS = 128
-KSLICES = 5
-LAGS = (0, 2, 4, 6, 8, 10, 14, 16, 18, 20)
-SLOTS = 8
+STORES = 8
+AHEAD = 4
+MATE_AT = 0
+KSLICES = 10
+LAGS = (0, 2, 4, 6, 8, 10, 14, 19, 25, 27)
 F32, BF16 = jnp.float32, jnp.bfloat16
 
 
 def _kernel(
     side, nc, x_hbm, wg_hbm, wu_hbm, wd_hbm, y,
-    wg, wu, wd, xb, h, p32, p16, got1, got2, fw1, fw2, t32, t16,
+    w, wd, xb, h, p32, p16, got1, got2, fw1, fw2, t32, t16,
     s1a, s1b, r1a, r1b, s2a, s2b, r2a, r2b, sg2a, sg2b, rg2a, rg2b, sg1a, sg1b, rg1a, rg1b, sd, rd, sh, rh, swd, rwd, lx, lw, lwd,
 ):
     R = xb.shape[1]
     K = xb.shape[2]
-    FF = wg.shape[1]
+    FF = w.shape[2]
     C = p32.shape[2]
     CB, CH = C // 2, C // 4
     R1, R2 = R // side, R // side // side
@@ -62,20 +64,18 @@
     def load_w(i):
         rows = pl.ds(i * KS, KS)
         return (
-            pltpu.make_async_copy(wg_hbm.at[rows, :], wg.at[rows, :], lw.at[0, i]),
-            pltpu.make_async_copy(wu_hbm.at[rows, :], wu.at[rows, :], lw.at[1, i]),
+            pltpu.make_async_copy(wg_hbm.at[rows, :], w.at[0, rows, :], lw.at[i % AHEAD]),
+            pltpu.make_async_copy(wu_hbm.at[rows, :], w.at[1, rows, :], lw.at[i % AHEAD]),
         )
 
     my_cols = pl.ds(pl.multiple_of(core * C, C), C)
     mate_cols = pl.ds(pl.multiple_of((1 - core) * C, C), C)
 
     load_x(0).start()
-    for i in range(KSLICES):
+    for i in range(AHEAD):
         for copy in load_w(i):
             copy.start()
     wd_own = pltpu.make_async_copy(wd_hbm.at[:, my_cols], wd.at[pl.ds(0, FF), :], lwd)
-    wd_own.start()
-    load_x(1).start()
 
     barrier = pltpu.get_barrier_semaphore()
     for d in (mate, xp, xm, yp, ym):
@@ -83,7 +83,6 @@
     pl.semaphore_wait(barrier, 5)
 
     wd_mate = remote(wd_hbm.at[:, mate_cols], wd.at[pl.ds(FF, FF), :], swd, rwd, mate)
-    wd_mate.start()
 
     def send_h(j):
         return remote(
@@ -98,8 +97,8 @@
         load_x(j).wait()
         for t in range(FF // TN):
             cols = pl.ds(t * TN, TN)
-            g = jnp.dot(xb[slot], wg[:, cols], preferred_element_type=F32)
-            u = jnp.dot(xb[slot], wu[:, cols], preferred_element_type=F32)
+            g = jnp.dot(xb[slot], w[0, :, cols], preferred_element_type=F32)
+            u = jnp.dot(xb[slot], w[1, :, cols], preferred_element_type=F32)
             h[turn(h, j), :, cols] = (jax.nn.silu(g) * u).astype(BF16)
         send_h(j).start()
 
@@ -110,11 +109,18 @@
     def gate_up_first():
         load_x(0).wait()
         for i in range(KSLICES):
-            for copy in load_w(i):
-                copy.wait()
             part = pl.ds(i * KS, KS)
-            g = jnp.dot(xb[0, :, part], wg[part, :], preferred_element_type=F32)
-            u = jnp.dot(xb[0, :, part], wu[part, :], preferred_element_type=F32)
+            pltpu.make_async_copy(w.at[:, part, :], w.at[:, part, :], lw.at[i % AHEAD]).wait()
+            if i == MATE_AT:
+                wd_mate.start()
+            if i + AHEAD < KSLICES:
+                for copy in load_w(i + AHEAD):
+                    copy.start()
+            elif i + AHEAD == KSLICES:
+                load_x(1).start()
+                wd_own.start()
+            g = jnp.dot(xb[0, :, part], w[0, part, :], preferred_element_type=F32)
+            u = jnp.dot(xb[0, :, part], w[1, part, :], preferred_element_type=F32)
             if i > 0:
                 g, u = p32[0, :, pl.ds(0, FF)] + g, p32[1, :, pl.ds(0, FF)] + u
             if i < KSLICES - 1:
@@ -249,9 +255,12 @@
         gathers(phase, j, 1).wait_recv()
         gathers(phase, j, 1).wait_send()
 
-    def swap(j, mine):
-        rows = pl.ds(pl.multiple_of(j * R, R), R)
-        block = y.at[rows, my_cols if mine else mate_cols]
+    def swap(j, k, dq):
+        block = y_block(1, j, k, ring[1][k][0] + dq)
+        return remote(block, block, sd.at[turn(sd, j)], rd.at[turn(rd, j)], mate)
+
+    def swaps(j):
+        block = y.at[pl.ds(pl.multiple_of(j * R, R), R), mate_cols]
         return remote(block, block, sd.at[turn(sd, j)], rd.at[turn(rd, j)], mate)
 
     def stage2(j):
@@ -270,13 +279,20 @@
         ag_end(2, j)
         ag_start(1, j)
 
+    def stage7(j):
+        ag_pass(1, j)
+        for dq in (-1, 0, 1):
+            for k in range(2):
+                swap(j, k, dq).start()
+
     def stage8(j):
         ag_end(1, j)
-        swap(j, True).start()
+        for k in range(2):
+            swap(j, k, 2).start()
 
     def stage9(j):
-        swap(j, True).wait_send()
-        swap(j, False).wait_recv()
+        swaps(j).wait_send()
+        swaps(j).wait_recv()
 
     stages = (
         None,
@@ -286,35 +302,55 @@
         stage4,
         functools.partial(ag_pass, 2),
         stage6,
-        functools.partial(ag_pass, 1),
+        stage7,
         stage8,
         stage9,
     )
 
     gate_up_first()
-    wd_own.wait()
-    wd_mate.wait()
 
     def step(s, carry):
-        for i in range(len(stages) - 1, 0, -1):
+        def run(i):
             j = s - LAGS[i]
 
             @pl.when(jnp.logical_and(j >= 0, j < nc))
             def _():
                 stages[i](j)
 
+        for i in range(len(stages) - 1, 1, -1):
+            run(i)
+
         @pl.when(s + 1 < nc)
         def _():
             gate_up(s + 1)
 
+        run(1)
+
         @pl.when(s < nc)
         def _():
+            @pl.when(s == 0)
+            def _():
+                wd_own.wait()
+                wd_mate.wait()
+
             down(s)
             rs_raw(1, s)
 
         return carry
 
     lax.fori_loop(0, nc + LAGS[-1], step, 0)
+
+
+def _store(y, out, sems):
+    size = y.shape[0] // STORES
+    copies = [
+        pltpu.make_async_copy(y.at[pl.ds(i * size, size), :], out.at[pl.ds(i * size, size), :], sems.at[i])
+        for i in range(STORES)
+    ]
+    for copy in copies:
+        copy.start()
+    for copy in copies:
+        copy.wait()
 
 
 def _mlp(side, x, w_gate, w_up, w_down):
@@ -334,27 +370,26 @@
         in_specs=[pl.BlockSpec(memory_space=pl.ANY)] * 4,
         out_specs=pl.BlockSpec(memory_space=pltpu.VMEM),
         scratch_shapes=[
-            pltpu.VMEM((depth, ff), BF16),
-            pltpu.VMEM((depth, ff), BF16),
+            pltpu.VMEM((2, depth, ff), BF16),
             pltpu.VMEM((2 * ff, C), BF16),
             pltpu.VMEM((2, R, depth), BF16),
             pltpu.VMEM((4, R, 2 * ff), BF16),
             pltpu.VMEM((L[2], R, C), F32),
             pltpu.VMEM((L[1], R, C), BF16),
-            pltpu.VMEM((SLOTS, 6, 2, R1, CH), BF16),
-            pltpu.VMEM((SLOTS, 6, 2, R2, CH), BF16),
+            pltpu.VMEM((2 * L[2] - L[1], 6, 2, R1, CH), BF16),
+            pltpu.VMEM((2 * L[4] - L[3] - L[2], 6, 2, R2, CH), BF16),
             pltpu.VMEM((L[2] - L[1], 2, 2, R1, CH), BF16),
             pltpu.VMEM((L[4] - L[3], 2, 2, R2, CH), BF16),
             pltpu.VMEM((L[4] - L[2], 2, R1, CB), F32),
             pltpu.VMEM((L[3] - L[2], 2, R1, CB), BF16),
-            dma((L[1],)), dma((L[2] - L[1],)), dma((SLOTS,)), dma((SLOTS,)),
-            dma((L[3] - L[2],)), dma((L[4] - L[3],)), dma((SLOTS,)), dma((SLOTS,)),
-            dma((L[5] - L[4],)), dma((L[6] - L[5],)), dma((SLOTS,)), dma((SLOTS,)),
-            dma((L[7] - L[6],)), dma((L[8] - L[7],)), dma((SLOTS,)), dma((SLOTS,)),
-            dma((L[9] - L[8],)), dma((SLOTS,)),
+            dma((L[1],)), dma((L[2] - L[1],)), dma((L[2],)), dma((2 * L[2] - L[1],)),
+            dma((L[3] - L[2],)), dma((L[4] - L[3],)), dma((L[4] - L[2],)), dma((2 * L[4] - L[3] - L[2],)),
+            dma((L[5] - L[4],)), dma((L[6] - L[5],)), dma((L[6] - L[4],)), dma((L[6] - L[5] + 2,)),
+            dma((L[7] - L[6],)), dma((L[8] - L[7],)), dma((L[8] - L[6],)), dma((L[8] - L[6],)),
+            dma((L[9] - L[7],)), dma((L[9] - L[7] + 2,)),
             dma((2,)), dma((4,)),
             dma, dma,
-            dma((2,)), dma((2, KSLICES)), dma,
+            dma((2,)), dma((AHEAD,)), dma,
         ],
         compiler_params=pltpu.CompilerParams(
             collective_id=0, has_side_effects=True, vmem_limit_bytes=43 * 1024 * 1024,
@@ -363,7 +398,15 @@
             flops=6 * rows * depth * ff, bytes_accessed=4 * rows * depth, transcendentals=rows * ff,
         ),
     )(x, w_gate, w_up, w_down)
-    return y
+    return pl.pallas_call(
+        _store,
+        out_shape=jax.ShapeDtypeStruct((rows, width), BF16),
+        in_specs=[pl.BlockSpec(memory_space=pl.ANY)],
+        out_specs=pl.BlockSpec(memory_space=pl.ANY),
+        scratch_shapes=[dma((STORES,))],
+        compiler_params=pltpu.CompilerParams(vmem_limit_bytes=1024 * 1024),
+        cost_estimate=pl.CostEstimate(flops=0, bytes_accessed=2 * rows * width, transcendentals=0),
+    )(pltpu.with_memory_space_constraint(y, pltpu.VMEM))
 
 
 def solution(mesh):

time: 137 us -> 132 us (0.964)
  local copies, waits for them, and re-layouts: 7.54 us -> 0 us
  Pallas kernels: 130 us -> 132 us
    unnamed x1 -> x0, local copies, waits for them, and re-layouts: 7.54 us -> none
    pallas_call x0 -> x1, Pallas kernels: none -> 7.23 us  [_mlp(): pl.pallas_call(_store, out_shape=jax.ShapeDtypeStruct((rows, width), BF16...]
    pallas_call x1, Pallas kernels: 130 us -> 125 us  [_mlp(): pl.pallas_call(functools.partial(_kernel, side, nc), out_shape=pltpu.VMEM...]
where the time goes in v3:
time: 132 us
  Pallas kernels  132 us (100%)
    pallas_call x1, Pallas kernels, _mlp(): pl.pallas_call(functools.partial(_kernel, side, nc), out_shape=pltpu.VMEM...  125 us
    pallas_call x1, Pallas kernels, _mlp(): pl.pallas_call(_store, out_shape=jax.ShapeDtypeStruct((rows, width), BF16...  7.23 us

profile of v3, /device:TPU:97, one launch (start us, length us, event | category | flops | bytes accessed | tf_op | source)
XLA Modules:
  0.0 132.2 jit_solution(2527958718515505551)
XLA Ops:
  0.0 125.0 %shard_map.46.y = bf16[2048,5120]{1,0:T(8,128)(2,1)S(1)} custom-call(bf16[2048,5120]{1,0:T(8,128)(2,1)} %x_hbm.1, bf16[5120,512]{1,0:T(8,128)(2,1)} %wg_hbm.1, bf16[5120,512]{1,0:T(8,128)(2,1)} %wu_hbm.1, bf16[512,5120]{1,0:T(8,128)(2,1)} %wd_hbm.1), custom_call_target="tpu_custom_call" | custom-call | flops 32212254720 | bytes 41943040 | tf_op jit(solution)/shard_map/pallas_call | solution.py:367
  125.0 7.2 %shard_map.47 = bf16[2048,5120]{1,0:T(8,128)(2,1)} custom-call(bf16[2048,5120]{1,0:T(8,128)(2,1)S(1)} %shard_map.46.y), custom_call_target="tpu_custom_call" | custom-call | bytes 20971520 | tf_op jit(solution)/shard_map/pallas_call | solution.py:401

commit v4 on v3

--- a/solution.py
+++ b/solution.py
@@ -11,17 +11,18 @@
 MESH = pl.DeviceIdType.MESH
 ROWS = 128
 STORES = 8
-AHEAD = 4
-MATE_AT = 0
+AHEAD = 3
+STAGGER = 4
+GAP = 250
 KSLICES = 10
-LAGS = (0, 2, 4, 6, 8, 10, 14, 19, 25, 27)
+LAGS = (0, 2, 4, 6, 8, 10, 14, 19, 25)
 F32, BF16 = jnp.float32, jnp.bfloat16
 
 
 def _kernel(
     side, nc, x_hbm, wg_hbm, wu_hbm, wd_hbm, y,
     w, wd, xb, h, p32, p16, got1, got2, fw1, fw2, t32, t16,
-    s1a, s1b, r1a, r1b, s2a, s2b, r2a, r2b, sg2a, sg2b, rg2a, rg2b, sg1a, sg1b, rg1a, rg1b, sd, rd, sh, rh, swd, rwd, lx, lw, lwd,
+    s1a, s1b, r1a, r1b, s2a, s2b, r2a, r2b, sy, rg2a, rg2b, rg1a, rg1b, rd, sh, rh, swd, rwd, lx, lw, lwd,
 ):
     R = xb.shape[1]
     K = xb.shape[2]
@@ -64,26 +65,30 @@
     def load_w(i):
         rows = pl.ds(i * KS, KS)
         return (
-            pltpu.make_async_copy(wg_hbm.at[rows, :], w.at[0, rows, :], lw.at[i % AHEAD]),
-            pltpu.make_async_copy(wu_hbm.at[rows, :], w.at[1, rows, :], lw.at[i % AHEAD]),
+            pltpu.make_async_copy(wg_hbm.at[rows, :], w.at[0, rows, :], lw.at[i % (AHEAD + STAGGER)]),
+            pltpu.make_async_copy(wu_hbm.at[rows, :], w.at[1, rows, :], lw.at[i % (AHEAD + STAGGER)]),
         )
 
     my_cols = pl.ds(pl.multiple_of(core * C, C), C)
     mate_cols = pl.ds(pl.multiple_of((1 - core) * C, C), C)
 
+    barrier = pltpu.get_barrier_semaphore()
+    for d in (mate, xp, xm, yp, ym):
+        pl.semaphore_signal(barrier, inc=1, device_id={"tp": d}, device_id_type=MESH)
     load_x(0).start()
     for i in range(AHEAD):
         for copy in load_w(i):
             copy.start()
     wd_own = pltpu.make_async_copy(wd_hbm.at[:, my_cols], wd.at[pl.ds(0, FF), :], lwd)
 
-    barrier = pltpu.get_barrier_semaphore()
-    for d in (mate, xp, xm, yp, ym):
-        pl.semaphore_signal(barrier, inc=1, device_id={"tp": d}, device_id_type=MESH)
+    for i in range(AHEAD, AHEAD + STAGGER):
+        pl.delay(GAP)
+        for copy in load_w(i):
+            copy.start()
     pl.semaphore_wait(barrier, 5)
 
     wd_mate = remote(wd_hbm.at[:, mate_cols], wd.at[pl.ds(FF, FF), :], swd, rwd, mate)
-
+    wd_mate.start()
     def send_h(j):
         return remote(
             h.at[turn(h, j), :, pl.ds(0, FF)], h.at[turn(h, j), :, pl.ds(FF, FF)],
@@ -110,13 +115,11 @@
         load_x(0).wait()
         for i in range(KSLICES):
             part = pl.ds(i * KS, KS)
-            pltpu.make_async_copy(w.at[:, part, :], w.at[:, part, :], lw.at[i % AHEAD]).wait()
-            if i == MATE_AT:
-                wd_mate.start()
-            if i + AHEAD < KSLICES:
-                for copy in load_w(i + AHEAD):
+            pltpu.make_async_copy(w.at[:, part, :], w.at[:, part, :], lw.at[i % (AHEAD + STAGGER)]).wait()
+            if i + AHEAD + STAGGER < KSLICES:
+                for copy in load_w(i + AHEAD + STAGGER):
                     copy.start()
-            elif i + AHEAD == KSLICES:
+            elif i + AHEAD + STAGGER == KSLICES:
                 load_x(1).start()
                 wd_own.start()
             g = jnp.dot(xb[0, :, part], w[0, part, :], preferred_element_type=F32)
@@ -224,20 +227,20 @@
         row = j * R + lax.rem(q + side, side) * R1
         return y.at[pl.ds(pl.multiple_of(row, R1), R1), cols]
 
-    gsem = {1: ((sg1a, sg1b), (rg1a, rg1b)), 2: ((sg2a, sg2b), (rg2a, rg2b))}
+    gsem = {1: (rg1a, rg1b), 2: (rg2a, rg2b)}
 
     def gather(phase, j, k, m):
-        ss, rs = (sems[m // 2] for sems in gsem[phase])
+        rs = gsem[phase][m // 2]
         q, np_, nm = ring[phase][k]
         dq, hf = ((0, None), (0, None), (-1, 0), (1, 1))[m]
         block = y_block(phase, j, k, q + dq, hf)
-        return remote(block, block, ss.at[turn(ss, j)], rs.at[turn(rs, j)], (np_, nm)[m % 2])
+        return remote(block, block, sy, rs.at[turn(rs, j)], (np_, nm)[m % 2])
 
     def gathers(phase, j, late):
-        ss, rs = (sems[late] for sems in gsem[phase])
+        rs = gsem[phase][late]
         size = (R1, R)[phase == 1] // (1 + late)
         block = y.at[pl.ds(pl.multiple_of(j * R, R), size), pl.ds(0, CB)]
-        return remote(block, block, ss.at[turn(ss, j)], rs.at[turn(rs, j)], mate)
+        return remote(block, block, sy, rs.at[turn(rs, j)], mate)
 
     def ag_start(phase, j):
         for m in range(2):
@@ -249,19 +252,13 @@
         for m in range(2):
             for k in range(2):
                 gather(phase, j, k, 2 + m).start()
-        gathers(phase, j, 0).wait_send()
 
     def ag_end(phase, j):
         gathers(phase, j, 1).wait_recv()
-        gathers(phase, j, 1).wait_send()
 
     def swap(j, k, dq):
         block = y_block(1, j, k, ring[1][k][0] + dq)
-        return remote(block, block, sd.at[turn(sd, j)], rd.at[turn(rd, j)], mate)
-
-    def swaps(j):
-        block = y.at[pl.ds(pl.multiple_of(j * R, R), R), mate_cols]
-        return remote(block, block, sd.at[turn(sd, j)], rd.at[turn(rd, j)], mate)
+        return remote(block, block, sy, rd, mate)
 
     def stage2(j):
         rs_finish(1, j, store_t(j))
@@ -289,10 +286,6 @@
         ag_end(1, j)
         for k in range(2):
             swap(j, k, 2).start()
-
-    def stage9(j):
-        swaps(j).wait_send()
-        swaps(j).wait_recv()
 
     stages = (
         None,
@@ -304,7 +297,6 @@
         stage6,
         stage7,
         stage8,
-        stage9,
     )
 
     gate_up_first()
@@ -339,6 +331,11 @@
         return carry
 
     lax.fori_loop(0, nc + LAGS[-1], step, 0)
+
+    half_y = y.at[:, mate_cols]
+    remote(half_y, half_y, sy, rd, mate).wait_recv()
+    sent = y.at[pl.ds(0, nc * (R + 3 * (R1 + R2)) // 2), :]
+    remote(sent, sent, sy, rd, mate).wait_send()
 
 
 def _store(y, out, sems):
@@ -384,12 +381,10 @@
             pltpu.VMEM((L[3] - L[2], 2, R1, CB), BF16),
             dma((L[1],)), dma((L[2] - L[1],)), dma((L[2],)), dma((2 * L[2] - L[1],)),
             dma((L[3] - L[2],)), dma((L[4] - L[3],)), dma((L[4] - L[2],)), dma((2 * L[4] - L[3] - L[2],)),
-            dma((L[5] - L[4],)), dma((L[6] - L[5],)), dma((L[6] - L[4],)), dma((L[6] - L[5] + 2,)),
-            dma((L[7] - L[6],)), dma((L[8] - L[7],)), dma((L[8] - L[6],)), dma((L[8] - L[6],)),
-            dma((L[9] - L[7],)), dma((L[9] - L[7] + 2,)),
+            dma, dma((L[6] - L[4],)), dma((L[6] - L[5] + 2,)), dma((L[8] - L[6],)), dma((L[8] - L[6],)), dma,
             dma((2,)), dma((4,)),
             dma, dma,
-            dma((2,)), dma((AHEAD,)), dma,
+            dma((2,)), dma((AHEAD + STAGGER,)), dma,
         ],
         compiler_params=pltpu.CompilerParams(
             collective_id=0, has_side_effects=True, vmem_limit_bytes=43 * 1024 * 1024,

time: 132 us -> 132 us (level)
  no operation moved by 1% of the time
where the time goes in v4:
time: 132 us; the launch traced here: 131 us
  Pallas kernels  131 us (99%)
    pallas_call x1, Pallas kernels, _mlp(): pl.pallas_call(functools.partial(_kernel, side, nc), out_shape=pltpu.VMEM...  124 us
    pallas_call x1, Pallas kernels, _mlp(): pl.pallas_call(_store, out_shape=jax.ShapeDtypeStruct((rows, width), BF16...  7.23 us

profile of v4, /device:TPU:97, one launch (start us, length us, event | category | flops | bytes accessed | tf_op | source)
XLA Modules:
  0.0 131.4 jit_solution(16942950809470293760)
XLA Ops:
  0.0 124.2 %shard_map.46.y = bf16[2048,5120]{1,0:T(8,128)(2,1)S(1)} custom-call(bf16[2048,5120]{1,0:T(8,128)(2,1)} %x_hbm.1, bf16[5120,512]{1,0:T(8,128)(2,1)} %wg_hbm.1, bf16[5120,512]{1,0:T(8,128)(2,1)} %wu_hbm.1, bf16[512,5120]{1,0:T(8,128)(2,1)} %wd_hbm.1), custom_call_target="tpu_custom_call" | custom-call | flops 32212254720 | bytes 41943040 | tf_op jit(solution)/shard_map/pallas_call | solution.py:364
  124.2 7.2 %shard_map.47 = bf16[2048,5120]{1,0:T(8,128)(2,1)} custom-call(bf16[2048,5120]{1,0:T(8,128)(2,1)S(1)} %shard_map.46.y), custom_call_target="tpu_custom_call" | custom-call | bytes 20971520 | tf_op jit(solution)/shard_map/pallas_call | solution.py:396

commit v5 on v4

--- a/solution.py
+++ b/solution.py
@@ -15,14 +15,14 @@
 STAGGER = 4
 GAP = 250
 KSLICES = 10
-LAGS = (0, 2, 4, 6, 8, 10, 14, 19, 25)
+LAGS = (0, 2, 4, 6, 8, 10, 15, 20, 26)
 F32, BF16 = jnp.float32, jnp.bfloat16
 
 
 def _kernel(
     side, nc, x_hbm, wg_hbm, wu_hbm, wd_hbm, y,
     w, wd, xb, h, p32, p16, got1, got2, fw1, fw2, t32, t16,
-    s1a, s1b, r1a, r1b, s2a, s2b, r2a, r2b, sy, rg2a, rg2b, rg1a, rg1b, rd, sh, rh, swd, rwd, lx, lw, lwd,
+    s1a, s1b, r1a, r1b, s2a, s2b, r2a, r2b, sy, rg2a, rg2b, rg1a, rg1b, rd, sh, rh, swd, rwd, lx, lwd,
 ):
     R = xb.shape[1]
     K = xb.shape[2]
@@ -65,8 +65,8 @@
     def load_w(i):
         rows = pl.ds(i * KS, KS)
         return (
-            pltpu.make_async_copy(wg_hbm.at[rows, :], w.at[0, rows, :], lw.at[i % (AHEAD + STAGGER)]),
-            pltpu.make_async_copy(wu_hbm.at[rows, :], w.at[1, rows, :], lw.at[i % (AHEAD + STAGGER)]),
+            pltpu.make_async_copy(wg_hbm.at[rows, :], w.at[0, rows, :], rg1b.at[i % (AHEAD + STAGGER)]),
+            pltpu.make_async_copy(wu_hbm.at[rows, :], w.at[1, rows, :], rg1b.at[i % (AHEAD + STAGGER)]),
         )
 
     my_cols = pl.ds(pl.multiple_of(core * C, C), C)
@@ -115,12 +115,13 @@
         load_x(0).wait()
         for i in range(KSLICES):
             part = pl.ds(i * KS, KS)
-            pltpu.make_async_copy(w.at[:, part, :], w.at[:, part, :], lw.at[i % (AHEAD + STAGGER)]).wait()
+            pltpu.make_async_copy(w.at[:, part, :], w.at[:, part, :], rg1b.at[i % (AHEAD + STAGGER)]).wait()
             if i + AHEAD + STAGGER < KSLICES:
                 for copy in load_w(i + AHEAD + STAGGER):
                     copy.start()
             elif i + AHEAD + STAGGER == KSLICES:
                 load_x(1).start()
+            if i == 8:
                 wd_own.start()
             g = jnp.dot(xb[0, :, part], w[0, part, :], preferred_element_type=F32)
             u = jnp.dot(xb[0, :, part], w[1, part, :], preferred_element_type=F32)
@@ -384,7 +385,7 @@
             dma, dma((L[6] - L[4],)), dma((L[6] - L[5] + 2,)), dma((L[8] - L[6],)), dma((L[8] - L[6],)), dma,
             dma((2,)), dma((4,)),
             dma, dma,
-            dma((2,)), dma((AHEAD + STAGGER,)), dma,
+            dma((2,)), dma,
         ],
         compiler_params=pltpu.CompilerParams(
             collective_id=0, has_side_effects=True, vmem_limit_bytes=43 * 1024 * 1024,

time: 132 us -> 131 us (level)
  no operation moved by 1% of the time
where the time goes in v5:
time: 131 us
  Pallas kernels  131 us (100%)
    pallas_call x1, Pallas kernels, _mlp(): pl.pallas_call(functools.partial(_kernel, side, nc), out_shape=pltpu.VMEM...  124 us
    pallas_call x1, Pallas kernels, _mlp(): pl.pallas_call(_store, out_shape=jax.ShapeDtypeStruct((rows, width), BF16...  7.23 us

profile of v5, /device:TPU:97, one launch (start us, length us, event | category | flops | bytes accessed | tf_op | source)
XLA Modules:
  0.0 131.4 jit_solution(8813128857298260854)
XLA Ops:
  0.0 124.1 %shard_map.46.y = bf16[2048,5120]{1,0:T(8,128)(2,1)S(1)} custom-call(bf16[2048,5120]{1,0:T(8,128)(2,1)} %x_hbm.1, bf16[5120,512]{1,0:T(8,128)(2,1)} %wg_hbm.1, bf16[5120,512]{1,0:T(8,128)(2,1)} %wu_hbm.1, bf16[512,5120]{1,0:T(8,128)(2,1)} %wd_hbm.1), custom_call_target="tpu_custom_call" | custom-call | flops 32212254720 | bytes 41943040 | tf_op jit(solution)/shard_map/pallas_call | solution.py:365
  124.2 7.2 %shard_map.47 = bf16[2048,5120]{1,0:T(8,128)(2,1)} custom-call(bf16[2048,5120]{1,0:T(8,128)(2,1)S(1)} %shard_map.46.y), custom_call_target="tpu_custom_call" | custom-call | bytes 20971520 | tf_op jit(solution)/shard_map/pallas_call | solution.py:397

commit v6 on v5

--- a/solution.py
+++ b/solution.py
@@ -22,7 +22,7 @@
 def _kernel(
     side, nc, x_hbm, wg_hbm, wu_hbm, wd_hbm, y,
     w, wd, xb, h, p32, p16, got1, got2, fw1, fw2, t32, t16,
-    s1a, s1b, r1a, r1b, s2a, s2b, r2a, r2b, sy, rg2a, rg2b, rg1a, rg1b, rd, sh, rh, swd, rwd, lx, lwd,
+    s1a, s1b, r1a, r1b, s2a, s2b, r2a, r2b, sy, rg2a, rg2b, rg1a, rg1b, rd, sh, rh, lx,
 ):
     R = xb.shape[1]
     K = xb.shape[2]
@@ -79,7 +79,7 @@
     for i in range(AHEAD):
         for copy in load_w(i):
             copy.start()
-    wd_own = pltpu.make_async_copy(wd_hbm.at[:, my_cols], wd.at[pl.ds(0, FF), :], lwd)
+    wd_own = pltpu.make_async_copy(wd_hbm.at[:, my_cols], wd.at[pl.ds(0, FF), :], s2b.at[0])
 
     for i in range(AHEAD, AHEAD + STAGGER):
         pl.delay(GAP)
@@ -87,7 +87,7 @@
             copy.start()
     pl.semaphore_wait(barrier, 5)
 
-    wd_mate = remote(wd_hbm.at[:, mate_cols], wd.at[pl.ds(FF, FF), :], swd, rwd, mate)
+    wd_mate = remote(wd_hbm.at[:, mate_cols], wd.at[pl.ds(FF, FF), :], s2a.at[0], r2b.at[0], mate)
     wd_mate.start()
     def send_h(j):
         return remote(
@@ -95,7 +95,7 @@
             sh.at[turn(sh, j)], rh.at[turn(rh, j)], mate,
         )
 
-    TN = min(256, FF)
+    TN = min(512, FF)
 
     def gate_up(j):
         slot = lax.rem(j, 2)
@@ -135,7 +135,7 @@
         send_h(0).start()
         load_x(2).start()
 
-    TD = 512 if C % 512 == 0 else CH
+    TD = CB
 
     def down(j):
         send_h(j).wait()
@@ -384,8 +384,7 @@
             dma((L[3] - L[2],)), dma((L[4] - L[3],)), dma((L[4] - L[2],)), dma((2 * L[4] - L[3] - L[2],)),
             dma, dma((L[6] - L[4],)), dma((L[6] - L[5] + 2,)), dma((L[8] - L[6],)), dma((L[8] - L[6],)), dma,
             dma((2,)), dma((4,)),
-            dma, dma,
-            dma((2,)), dma,
+            dma((2,)),
         ],
         compiler_params=pltpu.CompilerParams(
             collective_id=0, has_side_effects=True, vmem_limit_bytes=43 * 1024 * 1024,

time: 131 us -> 131 us (level)
  no operation moved by 1% of the time
where the time goes in v6:
time: 131 us
  Pallas kernels  131 us (100%)
    pallas_call x1, Pallas kernels, _mlp(): pl.pallas_call(functools.partial(_kernel, side, nc), out_shape=pltpu.VMEM...  124 us
    pallas_call x1, Pallas kernels, _mlp(): pl.pallas_call(_store, out_shape=jax.ShapeDtypeStruct((rows, width), BF16...  7.23 us

profile of v6, /device:TPU:97, one launch (start us, length us, event | category | flops | bytes accessed | tf_op | source)
XLA Modules:
  0.0 131.3 jit_solution(17435556735721360261)
XLA Ops:
  0.0 124.1 %shard_map.46.y = bf16[2048,5120]{1,0:T(8,128)(2,1)S(1)} custom-call(bf16[2048,5120]{1,0:T(8,128)(2,1)} %x_hbm.1, bf16[5120,512]{1,0:T(8,128)(2,1)} %wg_hbm.1, bf16[5120,512]{1,0:T(8,128)(2,1)} %wu_hbm.1, bf16[512,5120]{1,0:T(8,128)(2,1)} %wd_hbm.1), custom_call_target="tpu_custom_call" | custom-call | flops 32212254720 | bytes 41943040 | tf_op jit(solution)/shard_map/pallas_call | solution.py:365
  124.1 7.2 %shard_map.47 = bf16[2048,5120]{1,0:T(8,128)(2,1)} custom-call(bf16[2048,5120]{1,0:T(8,128)(2,1)S(1)} %shard_map.46.y), custom_call_target="tpu_custom_call" | custom-call | bytes 20971520 | tf_op jit(solution)/shard_map/pallas_call | solution.py:396
